TPU v7x, 256 devices: a whole 4x4x8 slice. The times are simulated.
256 devices in a mesh: ep: 16 (over y, x), tp: 16 (over z, core).
Axes of the slice: x: 4, y: 4, z: 8, core: 2. Of those that a mesh axis runs over, the one named last changes fastest.
Arguments:
- tokens: bfloat16 [1024, 7168], P('ep'), may hold values from -6 to 6
- gate_scores: float32 [1024, 8], P('ep'), may hold values from 0.1 to 1
- expert_ids: int32 [1024, 8], P('ep'), may hold values from 0 to 31, all different within a row; in each aligned block of 64 rows (0 to 63, 64 to 127, ...) at most 24 rows name the same one
- gate_weight: bfloat16 [32, 7168, 2048], P('ep', None, 'tp'), may hold values from -0.0625 to 0.0625
- up_weight: bfloat16 [32, 7168, 2048], P('ep', None, 'tp'), may hold values from -0.0625 to 0.0625
- down_weight: bfloat16 [32, 2048, 7168], P('ep', 'tp'), may hold values from -0.125 to 0.125
Outputs:
- mixed: bfloat16 [1024, 7168], P('ep', 'tp')
Inputs may be any that keep to these rules, and one draw needn't show every extreme that they name: `expert_ids`: each row names 8 different experts. Among the tokens of one group, no expert is named by more than 24 tokens, and in every draw some expert is named by exactly 24 of them.
All inputs are finite; a program needn't handle non-finite values.
Results may differ from a plain program's by a relative error of at most 0.02.
Values may be sent and summed in bfloat16 or wider, within the bound.
A program may use at most 192 MiB of HBM per device.

v0:
```python
import jax
import jax.numpy as jnp
from jax import lax
from jax.sharding import Mesh
from jax.sharding import PartitionSpec as P

TP = ("tp_0", "tp_1")


def sum_in_order(tiles, axes, turns):
    inside = tiles.shape[1:]
    tiles = tiles.reshape(*(lax.axis_size(a) for a in axes), *inside)
    tiles = jnp.moveaxis(tiles, turns, range(len(axes))).reshape(-1, *inside)
    for k in turns:
        tiles = lax.psum_scatter(tiles, axes[k], scatter_dimension=0, tiled=True)
    return tiles[0]


def in_blocks(array, dim, size):
    lengths = array.shape
    tiles = array.reshape(*lengths[:dim], size, lengths[dim] // size, *lengths[dim + 1 :])
    return jnp.moveaxis(tiles, dim, 0)


def sum_by_axis(array, axes, turns, dim):
    size = lax.axis_size(axes)
    return sum_in_order(in_blocks(array, dim, size), axes, turns)


def local(tokens, gate_scores, expert_ids, gate_weight, up_weight, down_weight):
    n_ep = lax.axis_size("ep")
    n_tp = lax.axis_size(TP)
    tok_count, width = tokens.shape
    choose = expert_ids.shape[1]
    exp_local = gate_weight.shape[0]
    experts = exp_local * n_ep
    capacity = min(tok_count, 3 * tok_count * choose // (2 * experts))
    share = width // n_tp
    expert_range = jnp.arange(experts)
    picked = jnp.sum(
        (expert_ids[:, :, None] == expert_range[None, None, :]).astype(jnp.int32), axis=1
    )
    rank = jnp.cumsum(picked, axis=0) - picked
    slot = jnp.take_along_axis(rank, expert_ids, axis=1)
    token_range = jnp.arange(tok_count)
    slot_range = jnp.arange(capacity)
    hits = (rank.T[:, None, :] == slot_range[None, :, None]) & (picked.T[:, None, :] > 0)
    found = jnp.any(hits, axis=2)
    index = jnp.where(
        found, jnp.sum(hits.astype(jnp.int32) * token_range[None, None, :], axis=2), tok_count
    )
    padded = jnp.concatenate([tokens, jnp.zeros((1, width), jnp.bfloat16)], axis=0)
    outgoing = padded[index].reshape(n_ep, exp_local, capacity, width)
    received = lax.all_to_all(outgoing, "ep", split_axis=0, concat_axis=0, tiled=True)
    gate = jnp.einsum("sjcd,jdf->sjcf", received, gate_weight, preferred_element_type=jnp.float32)
    upper = jnp.einsum("sjcd,jdf->sjcf", received, up_weight, preferred_element_type=jnp.float32)
    hidden = (jax.nn.silu(gate) * upper).astype(jnp.bfloat16)
    partial_value = jnp.einsum(
        "sjcf,jfd->sjcd", hidden, down_weight, preferred_element_type=jnp.float32
    )
    rounded = partial_value.astype(jnp.bfloat16)
    summed = sum_by_axis(rounded, TP, (1, 0), 3).astype(jnp.float32).astype(jnp.bfloat16)
    returned = lax.all_to_all(summed, "ep", split_axis=0, concat_axis=0, tiled=True)
    results = returned.reshape(experts * capacity, share)
    flat_index = expert_ids * capacity + slot
    chosen_rows = results[flat_index]
    weights = 2.5 * gate_scores / jnp.sum(gate_scores, axis=1, keepdims=True)
    mixed = jnp.einsum("tk,tkd->td", weights, chosen_rows.astype(jnp.float32))
    return mixed.astype(jnp.bfloat16)


def solution(mesh):
    torus = Mesh(mesh.devices.reshape(mesh.shape["ep"], 8, 2), ("ep", "tp_0", "tp_1"))
    return jax.shard_map(
        local,
        mesh=torus,
        in_specs=(
            P("ep", None),
            P("ep", None),
            P("ep", None),
            P("ep", None, TP),
            P("ep", None, TP),
            P("ep", TP, None),
        ),
        out_specs=P("ep", TP),
        check_vma=False,
    )
```

profile of v0, /device:TPU:1, one launch (start us, length us, event | category | flops | bytes accessed | tf_op | source)
XLA Modules:
  0.0 362.8 jit_solution(16210950039114955713)
XLA Ops:
  6.5 0.0 reduce-scatter.3.cloned.1.call-start
  6.5 0.7 convert_reduce_fusion
  7.3 0.1 copy.49
  7.3 0.1 reduce_window_sum.11
  7.4 0.1 copy.51
  7.5 0.6 select_reduce_fusion
  8.1 0.6 fusion.40
  8.8 0.1 reshape.59
  8.9 1.2 concatenate.3
  10.1 9.5 %gather_fusion = bf16[768,7168]{1,0:T(8,128)(2,1)} fusion(bf16[65,7168]{1,0:T(8,128)(2,1)S(1)} %concatenate.3, s32[1024]{0:T(1024)S(1)} %pad_clamp_fusion.1), kind=kCustom, calls=%fused_computation | custom fusion | bytes 22023168 | tf_op jit(solution)/shard_map/gather | solution.py:53
  19.6 130.3 %all_to_all.10 = bf16[16,2,24,7168]{3,2,1,0:T(8,128)(2,1)S(1)} all-to-all(bf16[16,2,24,7168]{3,2,1,0:T(8,128)(2,1)} %bitcast.75), channel_id=1, replica_groups=mesh['ep'=16,'tp_0'=8,'tp_1'=2] {'ep'}, dimensions={0} | all-to-all | bytes 22020096 | tf_op jit(solution)/shard_map/all_to_all | solution.py:54
  150.0 0.0 copy-start
  150.0 4.2 %copy-done = bf16[16,2,24,7168]{3,2,1,0:T(8,128)(2,1)} copy-done((bf16[16,2,24,7168]{3,2,1,0:T(8,128)(2,1)}, bf16[16,2,24,7168]{3,2,1,0:T(8,128)(2,1)S(1)}, u32[]{:S(2)}) %copy-start) | copy-done | bytes 11010072
  154.1 5.0 %fusion.8 = f32[16,2,24,128]{3,2,0,1:T(8,128)S(1)} fusion(bf16[2,7168,128]{2,1,0:T(8,128)(2,1)} %param.9, bf16[16,2,24,7168]{3,2,1,0:T(8,128)(2,1)S(1)} %all_to_all.10), kind=kOutput, calls=%fused_computation.12 | convolution fusion | flops 1409286144 | bytes 15073280 | tf_op jit(solution)/shard_map/sjcd,jdf->sjcf/dot_general | solution.py:55
  159.2 13.2 %fusion = bf16[16,2,24,7168]{3,2,0,1:T(8,128)(2,1)} fusion(bf16[2,128,7168]{2,1,0:T(8,128)(2,1)} %param.11, bf16[2,7168,128]{2,1,0:T(8,128)(2,1)} %param.10, bf16[16,2,24,7168]{3,2,1,0:T(8,128)(2,1)} %copy-done, f32[16,2,24,128]{3,2,0,1:T(8,128)S(1)} %fusion.8), kind=kOutput, calls=%fused_computation.4 | convolution fusion | flops 2824667136 | bytes 29753344 | tf_op jit(solution)/shard_map/sjcf,jfd->sjcd/dot_general | solution.py:58
  172.4 21.7 %reshape.52 = bf16[16,2,24,16,448]{4,3,2,0,1:T(8,128)(2,1)} reshape(bf16[16,2,24,7168]{3,2,0,1:T(8,128)(2,1)} %fusion) | data formatting | bytes 22020096 | tf_op jit(solution)/shard_map/reshape | solution.py:21
  194.1 19.3 %reshape.53 = bf16[8,2,16,2,24,448]{5,1,0,4,2,3:T(2,128)(2,1)} reshape(bf16[16,16,2,24,448]{4,0,3,1,2:T(8,128)(2,1)} %bitcast.73) | data formatting | bytes 22020096 | tf_op jit(solution)/shard_map/reshape | solution.py:12
  213.4 13.0 %copy.54 = bf16[2,8,16,2,24,448]{5,4,3,2,1,0:T(8,128)(2,1)} copy(bf16[2,8,16,2,24,448]{5,0,1,4,2,3:T(2,128)(2,1)} %bitcast.74) | data formatting | bytes 22020096 | tf_op jit(solution)/shard_map/transpose | solution.py:13
  226.4 0.0 copy-start.1
  226.4 0.0 reduce-scatter.3.cloned.1.call-update
  226.4 0.0 reduce-scatter.5.cloned.1.call-start
  226.5 27.2 %reduce-scatter.3.cloned.1.call-done = bf16[8,16,2,24,448]{4,3,2,1,0:T(8,128)(2,1)} async-done(((bf16[16,16,2,24,448]{4,3,2,1,0:T(8,128)(2,1)}), bf16[8,16,2,24,448]{4,3,2,1,0:T(8,128)(2,1)}) %reduce-scatter.3.cloned.1.call-update) | async-done | bytes 5505040 | tf_op jit(solution)/shard_map/reduce_scatter | solution.py:15
  253.7 0.0 reduce-scatter.5.cloned.1.call-update
  253.7 79.6 %reduce-scatter.5.cloned.1.call-done = bf16[1,16,2,24,448]{4,3,2,1,0:T(8,128)(2,1)} async-done(((bf16[8,16,2,24,448]{4,3,2,1,0:T(8,128)(2,1)}), bf16[1,16,2,24,448]{4,3,2,1,0:T(8,128)(2,1)}) %reduce-scatter.5.cloned.1.call-update) | async-done | bytes 688144 | tf_op jit(solution)/shard_map/reduce_scatter | solution.py:15
  333.3 6.5 %all-to-all-start.1 = ((bf16[16,2,24,448]{3,2,1,0:T(8,128)(2,1)}), bf16[16,2,24,448]{3,2,1,0:T(8,128)(2,1)S(1)}, u32[]{:S(2)}, u32[]{:S(2)}) async-start(bf16[16,2,24,448]{3,2,1,0:T(8,128)(2,1)} %bitcast.77), calls=%async_computation.3 | async-start | bytes 1572864 | tf_op jit(solution)/shard_map/all_to_all | solution.py:63
  339.8 0.0 copy-done.1
  339.9 0.1 copy.55
  339.9 0.1 reshape.73
  340.0 0.0 copy-start.2
  340.0 3.8 %gather_fusion.2 = s32[512]{0:T(512)S(1)} fusion(s32[64,32]{1,0:T(8,128)S(1)} %sub.7, s32[512]{0:T(512)S(1)} %reshape.73), kind=kCustom, calls=%fused_computation.2 | custom fusion | bytes 8192 | tf_op jit(solution)/shard_map/jit(take_along_axis)/gather | solution.py:44
  343.8 0.1 reshape.76
  343.9 0.1 copy.56
  344.0 0.1 copy.57
  344.1 0.1 reshape.67
  344.2 0.0 copy-done.2
  344.2 0.1 copy.61
  344.3 8.7 %all-to-all-done.1 = bf16[16,2,24,448]{3,2,1,0:T(8,128)(2,1)S(1)} async-done(((bf16[16,2,24,448]{3,2,1,0:T(8,128)(2,1)}), bf16[16,2,24,448]{3,2,1,0:T(8,128)(2,1)S(1)}, u32[]{:S(2)}, u32[]{:S(2)}) %all-to-all-start.1) | async-done | bytes 688160 | tf_op jit(solution)/shard_map/all_to_all | solution.py:63
  353.0 2.0 gather_fusion.1
  355.0 0.3 fusion.32
  355.3 0.6 copy.78
  (9 shorter events, 0.1 us)
Async XLA Ops:
  6.5 247.2 %reduce-scatter.3.cloned.1.call-start = ((), (), s32[]{:S(2)}) async-start(), calls=%async_computation.4 | async-start | bytes 18874368 | tf_op jit(solution)/shard_map/reduce_scatter | solution.py:15
  150.0 4.2 %copy-start = (bf16[16,2,24,7168]{3,2,1,0:T(8,128)(2,1)}, bf16[16,2,24,7168]{3,2,1,0:T(8,128)(2,1)S(1)}, u32[]{:S(2)}) copy-start(bf16[16,2,24,7168]{3,2,1,0:T(8,128)(2,1)S(1)} %all_to_all.10) | copy-start | bytes 33030148
  226.4 113.4 %copy-start.1 = (s32[64,8]{0,1:T(8,128)S(1)}, s32[64,8]{0,1:T(8,128)}, u32[]{:S(2)}) copy-start(s32[64,8]{0,1:T(8,128)} %param.8) | copy-start | bytes 6148
  226.4 106.9 %reduce-scatter.5.cloned.1.call-start = ((), (), s32[]{:S(2)}) async-start(), calls=%async_computation.5 | async-start | bytes 7077888 | tf_op jit(solution)/shard_map/reduce_scatter | solution.py:15
  333.3 19.7 %all-to-all-start.1 = ((bf16[16,2,24,448]{3,2,1,0:T(8,128)(2,1)}), bf16[16,2,24,448]{3,2,1,0:T(8,128)(2,1)S(1)}, u32[]{:S(2)}, u32[]{:S(2)}) async-start(bf16[16,2,24,448]{3,2,1,0:T(8,128)(2,1)} %bitcast.77), calls=%async_computation.3 | async-start | bytes 1572864 | tf_op jit(solution)/shard_map/all_to_all | solution.py:63
  340.0 4.1 %copy-start.2 = (f32[64,8]{0,1:T(8,128)S(1)}, f32[64,8]{0,1:T(8,128)}, u32[]{:S(2)}) copy-start(f32[64,8]{0,1:T(8,128)} %param.7) | copy-start | bytes 6148
Sparse Core Ops, SparseCore 0:
  226.5 27.1 reduce-scatter.2
  256.3 76.9 reduce-scatter.4
where the time goes:
time: 364 us; the launch traced here: 363 us
  blocking collectives  130 us (36%)
  waiting for transfers between devices  116 us (32%)
  local copies, waits for them, and re-layouts  76.1 us (21%)
  matrix products  18.5 us (5%)
  between operations  13.5 us (4%)
  starting transfers between devices  6.57 us (2%)
    all_to_all x1, blocking collectives, local(): lax.all_to_all(outgoing, 'ep', split_axis=0, concat_axis=0, tiled=True)  130 us
    reduce_scatter x2, waiting for transfers between devices, sum_in_order(): tiles = lax.psum_scatter(tiles, axes[k], scatter_dimension=0, tiled=True)  107 us
    reshape x1, local copies, waits for them, and re-layouts, in_blocks(): array.reshape(*lengths[:dim], size, lengths[dim] // size, *lengths[dim +...  21.7 us
    reshape x1, local copies, waits for them, and re-layouts, sum_in_order(): tiles = tiles.reshape(*(lax.axis_size(a) for a in axes), *inside)  19.3 us
    dot_general x1, matrix products, local(): jnp.einsum('sjcf,jfd->sjcd', hidden, down_weight, preferred_element_type=...  13.2 us
    transpose x1, local copies, waits for them, and re-layouts, sum_in_order(): tiles = jnp.moveaxis(tiles, turns, range(len(axes))).reshape(-1, *inside)  13 us
    gather x1, local copies, waits for them, and re-layouts, local(): outgoing = padded[index].reshape(n_ep, exp_local, capacity, width)  9.47 us
    all_to_all x1, waiting for transfers between devices, local(): lax.all_to_all(summed, 'ep', split_axis=0, concat_axis=0, tiled=True)  8.68 us
  transfers between devices with their start and end apart: 3, of which 3 were waited for; matrix products, arithmetic and copies ran while one was open for 1% of the time, Pallas kernels for 0%

commit v1 on v0

v1 whole, which is shorter than its diff:
```python
import jax
import jax.numpy as jnp
from jax import lax
from jax.experimental import pallas as pl
from jax.experimental.pallas import tpu as pltpu
from jax.sharding import Mesh
from jax.sharding import PartitionSpec as P

F32, BF16 = jnp.float32, jnp.bfloat16
HALF = 3584
PART = 1280
ZOFF = 2 * PART
NA, NB = 384, 256
COPIES = 224


def kernel(
    tok, score, ids, gate_w, up_w, down_w, out,
    xa, xb, xc, wgu, wd, acc, wsend, wrecv, wcol, hid,
    ca, cb, cc, r1a, r2a, t1a, t2a, za, r1b, r2b, t1b, t2b, zb, q1, q2, q3, q4, xcr,
    send, recv, loc,
):
    y, x = lax.axis_index("y"), lax.axis_index("x")
    z, c = lax.axis_index("z"), lax.axis_index("c")
    g = y * 4 + x
    oc = 1 - c

    def m4(v, d):
        return lax.rem(v + (4 + d), 4)

    def m8(v, d):
        return lax.rem(v + (8 + d), 8)

    def dev(dy=0, dx=0, dz=0):
        return (m4(y, dy), m4(x, dx), m8(z, dz), c)

    sibling = (y, x, z, oc)
    started = []

    def put(src, dst, device):
        n = len(started)
        copy = pltpu.make_async_remote_copy(
            src_ref=src, dst_ref=dst, send_sem=send.at[n], recv_sem=recv.at[n],
            device_id=device, device_id_type=pl.DeviceIdType.MESH,
        )
        copy.start()
        started.append(copy)
        return copy

    def lanes(start, size):
        return pl.ds(pl.multiple_of(start, 128), size)

    plane = [(dy, dx) for dy in range(4) for dx in range(4) if dy or dx]

    own = [
        pltpu.make_async_copy(tok.at[:, lanes(c * HALF + ZOFF + z * 128, 128)], xc.at[c, z, g], loc.at[0]),
        pltpu.make_async_copy(tok.at[:, lanes(c * HALF, PART)], xa.at[c, y, x], loc.at[1]),
        pltpu.make_async_copy(tok.at[:, lanes(c * HALF + PART, PART)], xb.at[c, x, y], loc.at[2]),
    ]
    loads = []
    for e in range(2):
        loads.append(pltpu.make_async_copy(gate_w.at[e], wgu.at[:, pl.ds(e * 256, 128)], loc.at[3 + 3 * e]))
        loads.append(pltpu.make_async_copy(up_w.at[e], wgu.at[:, pl.ds(e * 256 + 128, 128)], loc.at[4 + 3 * e]))
        loads.append(pltpu.make_async_copy(down_w.at[e], wd.at[c, pl.ds(e * 128, 128)], loc.at[5 + 3 * e]))
    for copy in own:
        copy.start()

    barrier = pltpu.get_barrier_semaphore()
    for dy, dx in plane:
        pl.semaphore_signal(barrier, inc=1, device_id=dev(dy, dx), device_id_type=pl.DeviceIdType.MESH)
    for d in range(1, 8):
        pl.semaphore_signal(barrier, inc=1, device_id=dev(dz=d), device_id_type=pl.DeviceIdType.MESH)
    pl.semaphore_signal(barrier, inc=1, device_id=sibling, device_id_type=pl.DeviceIdType.MESH)
    for copy in own:
        copy.wait()
    for copy in loads:
        copy.start()
    pl.semaphore_wait(barrier, 23)

    routes = (
        (xa, y, x, lambda d: dev(dx=d), lambda d: dev(dy=d), 0, lambda k, j: k * 4 + j),
        (xb, x, y, lambda d: dev(dy=d), lambda d: dev(dx=d), PART, lambda k, j: j * 4 + k),
    )
    piece = {s: put(xc.at[c, z, g], xc.at[c, z, g], dev(*s)) for s in plane}
    first, half1, full2, half2 = {}, {}, {}, {}
    for p, (buf, k, i, m1, m2, off, rows) in enumerate(routes):
        for d in (1, -1):
            first[p, d] = put(buf.at[c, k, i], buf.at[c, k, i], m1(d))
    for p, (buf, k, i, m1, m2, off, rows) in enumerate(routes):
        for d in (1, -1):
            full2[p, 0, d] = put(buf.at[c, k, i], buf.at[c, k, i], m2(d))
    down_sib = [put(down_w.at[e], wd.at[c, pl.ds(e * 128, 128)], sibling) for e in range(2)]

    lane = lax.broadcasted_iota(jnp.int32, (64, 128), 1)
    expert = jnp.where((lane & 7) < 2, (lane >> 3) * 2 + (lane & 7), -1)
    s = score[...]
    norm = 2.5 * s / jnp.sum(s, axis=1, keepdims=True)
    dense = jnp.zeros((64, 128), F32)
    for t in range(8):
        dense += jnp.where(ids[:, t : t + 1] == expert, norm[:, t : t + 1], 0.0)
    wsend[...] = jnp.concatenate([dense, jnp.zeros((64, 128), F32)], axis=0).T.reshape(16, 8, 128)
    acc[...] = jnp.zeros_like(acc)
    wrecv[g] = wsend[g]
    wput = []
    for dy, dx in plane:
        to = m4(y, dy) * 4 + m4(x, dx)
        wput.append(put(wsend.at[to], wrecv.at[g], dev(dy, dx)))

    def mul(p, h, k):
        buf, off, rows = routes[p][0], routes[p][5], routes[p][6]
        start = pl.multiple_of(h * HALF + off, 128)
        r = jnp.dot(buf[h, k].reshape(256, PART), wgu[pl.ds(start, PART), :], preferred_element_type=F32)
        for j in range(4):
            acc[rows(k, j)] += r[j * 64 : (j + 1) * 64]

    def mulz(h, zz):
        start = pl.multiple_of(h * HALF + ZOFF + zz * 128, 128)

        @pl.loop(0, 4)
        def _(q):
            r = jnp.dot(xc[h, zz, pl.ds(q * 4, 4)].reshape(256, 128), wgu[pl.ds(start, 128), :], preferred_element_type=F32)
            acc[pl.ds(q * 4, 4)] += r.reshape(4, 64, 512)

    for s in plane:
        piece[s].wait_recv()
    zput = {(0, d): put(xc.at[c, z], xc.at[c, z], dev(dz=d)) for d in (1, -1)}
    zsib = [(put(xc.at[c, z], xc.at[c, z], sibling), z)]
    rsib = []

    for p, (buf, k, i, m1, m2, off, rows) in enumerate(routes):
        first[p, 1].wait_recv()
        b = m4(i, -1)
        half1[p, 1] = put(buf.at[c, k, b, pl.ds(0, 32)], buf.at[c, k, b, pl.ds(0, 32)], m1(1))
        first[p, -1].wait_recv()
        b = m4(i, 1)
        half1[p, -1] = put(buf.at[c, k, b, pl.ds(32, 32)], buf.at[c, k, b, pl.ds(32, 32)], m1(-1))
    for b in (-1, 1):
        for p, (buf, k, i, m1, m2, off, rows) in enumerate(routes):
            for d in (1, -1):
                full2[p, b, d] = put(buf.at[c, k, m4(i, b)], buf.at[c, k, m4(i, b)], m2(d))
    for copy in loads:
        copy.wait()
    mulz(c, z)
    for copy in wput:
        copy.wait_recv()
    wt = wrecv[...].reshape(128, 128).T
    wcol[...] = jnp.zeros_like(wcol)

    @pl.loop(0, 16)
    def _(q):
        for e in range(2):
            col = jnp.sum(jnp.where(lane == q * 8 + e, wt[:64], 0.0), axis=1, keepdims=True)
            wcol[q, :, e * 128 : (e + 1) * 128] = jnp.broadcast_to(col, (64, 128))

    def finish(p, k):
        buf = routes[p][0]
        rsib.append((put(buf.at[c, k], buf.at[c, k], sibling), p, k))
        mul(p, c, k)

    for p, (buf, k, i, m1, m2, off, rows) in enumerate(routes):
        half1[p, 1].wait_recv()
        half1[p, -1].wait_recv()
        for d in (1, -1):
            full2[p, 2, d] = put(buf.at[c, k, m4(i, 2)], buf.at[c, k, m4(i, 2)], m2(d))
    for p in range(2):
        finish(p, routes[p][1])

    def pass_on(b):
        for p, (buf, k, i, m1, m2, off, rows) in enumerate(routes):
            full2[p, b, 1].wait_recv()
            ref = buf.at[c, m4(k, -1), m4(i, b), pl.ds(0, 32)]
            half2[p, b, 1] = put(ref, ref, m2(1))
            full2[p, b, -1].wait_recv()
            ref = buf.at[c, m4(k, 1), m4(i, b), pl.ds(32, 32)]
            half2[p, b, -1] = put(ref, ref, m2(-1))

    def z_step(t):
        for d in (1, -1):
            zput[t - 1, d].wait_recv()
            zz = m8(z, -d * t)
            if t < 3:
                zput[t, d] = put(xc.at[c, zz], xc.at[c, zz], dev(dz=d))
            elif t == 3:
                part = pl.ds(0 if d == 1 else 8, 8)
                zput[t, d] = put(xc.at[c, zz, part], xc.at[c, zz, part], dev(dz=d))
            if t < 4:
                zsib.append((put(xc.at[c, zz], xc.at[c, zz], sibling), zz))
                mulz(c, zz)
        if t == 4:
            zz = m8(z, 4)
            zsib.append((put(xc.at[c, zz], xc.at[c, zz], sibling), zz))
            mulz(c, zz)

    def from_sib(n):
        copy, p, k = rsib[n]
        copy.wait_recv()
        mul(p, oc, k)

    def z_from_sib(n):
        copy, zz = zsib[n]
        copy.wait_recv()
        mulz(oc, zz)

    pass_on(0)
    z_step(1)
    z_from_sib(0)
    from_sib(0)
    from_sib(1)
    pass_on(-1)
    z_from_sib(1)
    z_from_sib(2)
    z_step(2)
    pass_on(1)
    z_from_sib(3)
    z_from_sib(4)
    pass_on(2)
    for p in range(2):
        finish(p, m4(routes[p][1], -1))
        finish(p, m4(routes[p][1], 1))
    z_step(3)
    for n in range(2, 6):
        from_sib(n)
    z_from_sib(5)
    z_from_sib(6)
    for p in range(2):
        for b in (0, -1, 1, 2):
            half2[p, b, 1].wait_recv()
            half2[p, b, -1].wait_recv()
        finish(p, m4(routes[p][1], 2))
    z_step(4)
    from_sib(6)
    from_sib(7)
    z_from_sib(7)

    @pl.loop(0, 16)
    def _(q):
        for e in range(2):
            gate = acc[q, :, e * 256 : e * 256 + 128]
            upper = acc[q, :, e * 256 + 128 : e * 256 + 256]
            value = gate / (1.0 + jnp.exp(-gate)) * upper * wcol[q, :, e * 128 : (e + 1) * 128]
            value = value.astype(BF16)
            hid[c, 0, q, :, e * 128 : (e + 1) * 128] = value[:32]
            hid[c, 1, q, :, e * 128 : (e + 1) * 128] = value[32:]

    hid_sib = put(hid.at[c], hid.at[c], sibling)
    for copy in down_sib:
        copy.wait_recv()
    hid_sib.wait_recv()

    ka, kb = y * oc + x * c, x * oc + y * c

    def along(first_axis, d):
        if first_axis:
            return (m4(y, 0) if d == 0 else lax.rem(y + 4 + d * c, 4), lax.rem(x + 4 + d * oc, 4), z, c)
        return (lax.rem(y + 4 + d * oc, 4), lax.rem(x + 4 + d * c, 4), z, c)

    def down(left, right, start, size):
        return jnp.dot(left, wd[0, :, lanes(start, size)], preferred_element_type=F32) + jnp.dot(
            right, wd[1, :, lanes(start, size)], preferred_element_type=F32
        )

    sums = (
        (ca, r1a, r2a, t1a, t2a, za, ka, kb, 0, NA, lambda d: along(False, d), lambda d: along(True, d),
         lambda k, j: (k * 4 + j) * oc + (j * 4 + k) * c),
        (cb, r1b, r2b, t1b, t2b, zb, kb, ka, 1, NB, lambda d: along(True, d), lambda d: along(False, d),
         lambda k, j: (j * 4 + k) * oc + (k * 4 + j) * c),
    )

    def row(p, k):
        buf, part, size, where = sums[p][0], sums[p][8], sums[p][9], sums[p][12]
        left = jnp.concatenate([hid[0, part, where(k, j)] for j in range(4)], axis=0)
        right = jnp.concatenate([hid[1, part, where(k, j)] for j in range(4)], axis=0)
        for zz in range(8):
            r = down(left, right, zz * 896 + c * 512, size)
            buf[k, :, :, zz * size : (zz + 1) * size] = r.reshape(4, 32, size).astype(BF16)

    side = (lax.broadcasted_iota(jnp.int32, (256, 128), 1) < 64) == (c == 0)

    def column(zz):
        @pl.loop(0, 2)
        def _(q):
            some = pl.ds(q * 8, 8)
            lo = [hid[n, 0, some].reshape(256, 256) for n in range(2)]
            hi = [hid[n, 1, some].reshape(256, 256) for n in range(2)]
            r = down(hi[0], hi[1], zz * 896 + c * 512 + 256, 128)
            cc[zz, some, :, 0:128] = r.reshape(8, 32, 128).astype(BF16)
            r_lo = down(lo[0], lo[1], zz * 896 + 384, 128)
            r_hi = down(hi[0], hi[1], zz * 896 + 384, 128)
            r = jnp.where(side, r_lo, pltpu.roll(r_hi, 64, 1))
            cc[zz, some, :, 128:256] = r.reshape(8, 32, 128).astype(BF16)

    def add(*refs):
        total = refs[0][...].astype(F32)
        for ref in refs[1:]:
            total += ref[...].astype(F32)
        refs[0][...] = total.astype(BF16)

    top, bottom = pl.ds(0, 16), pl.ds(16, 16)
    st1, ind, dep, st2, ind2, dep2 = {}, {}, {}, {}, {}, {}
    for p, (buf, r1, r2, t1, t2, zr, k, i, part, size, m2, m1, where) in enumerate(sums):
        row(p, m4(k, 2))
        st1[p, 1] = put(buf.at[m4(k, 2), :, top], r1.at[0], m2(1))
        st1[p, -1] = put(buf.at[m4(k, 2), :, bottom], r1.at[1], m2(-1))
    column(m8(z, 4))
    zq = {
        (1, 1): put(cc.at[m8(z, 4), pl.ds(0, 8)], q1.at[0], dev(dz=1)),
        (1, -1): put(cc.at[m8(z, 4), pl.ds(8, 8)], q1.at[1], dev(dz=-1)),
    }
    for p, (buf, r1, r2, t1, t2, zr, k, i, part, size, m2, m1, where) in enumerate(sums):
        row(p, m4(k, 1))
        ind[p, 1] = put(buf.at[m4(k, 1), :, bottom], r2.at[0, :, bottom], m2(1))
        row(p, m4(k, -1))
        ind[p, -1] = put(buf.at[m4(k, -1), :, top], r2.at[1, :, top], m2(-1))
    column(m8(z, 3))
    zi = {1: put(cc.at[m8(z, 3), pl.ds(8, 8)], q2.at[0, pl.ds(8, 8)], dev(dz=1))}
    column(m8(z, -3))
    zi[-1] = put(cc.at[m8(z, -3), pl.ds(0, 8)], q2.at[1, pl.ds(0, 8)], dev(dz=-1))

    zq[1, 1].wait_recv()
    add(cc.at[m8(z, 3), pl.ds(0, 8)], q1.at[0])
    zq[2, 1] = put(cc.at[m8(z, 3), pl.ds(0, 8)], q2.at[0, pl.ds(0, 8)], dev(dz=1))
    zq[1, -1].wait_recv()
    add(cc.at[m8(z, -3), pl.ds(8, 8)], q1.at[1])
    zq[2, -1] = put(cc.at[m8(z, -3), pl.ds(8, 8)], q2.at[1, pl.ds(8, 8)], dev(dz=-1))
    for t in (2, -2, 1, -1):
        column(m8(z, t))
    column(z)

    order = (2, 1, -1, 0)
    for p, (buf, r1, r2, t1, t2, zr, k, i, part, size, m2, m1, where) in enumerate(sums):
        st1[p, 1].wait_recv()
        st1[p, -1].wait_recv()
        for b in order:
            j = m4(i, b)
            add(buf.at[m4(k, 1), j, top], r1.at[0, j])
            dep[p, b, 1] = put(buf.at[m4(k, 1), j, top], r2.at[0, j, top], m2(1))
            add(buf.at[m4(k, -1), j, bottom], r1.at[1, j])
            dep[p, b, -1] = put(buf.at[m4(k, -1), j, bottom], r2.at[1, j, bottom], m2(-1))
    for p in range(2):
        row(p, sums[p][6])

    for n, d in enumerate((1, -1)):
        zi[d].wait_recv()
        zq[2, d].wait_recv()
        add(cc.at[m8(z, 2 * d)], q2.at[n])
        zq[3, d] = put(cc.at[m8(z, 2 * d)], q3.at[n], dev(dz=d))
    for n, d in enumerate((1, -1)):
        zq[3, d].wait_recv()
        add(cc.at[m8(z, d)], q3.at[n])
        zq[4, d] = put(cc.at[m8(z, d)], q4.at[n], dev(dz=d))

    for p in range(2):
        for d in (1, -1):
            ind[p, d].wait_recv()
    for b in order:
        for p, (buf, r1, r2, t1, t2, zr, k, i, part, size, m2, m1, where) in enumerate(sums):
            dep[p, b, 1].wait_recv()
            dep[p, b, -1].wait_recv()
            j = m4(i, b)
            add(buf.at[k, j], r2.at[0, j], r2.at[1, j])
            if b == 2:
                st2[p, 1] = put(buf.at[k, j, top], t1.at[0], m1(1))
                st2[p, -1] = put(buf.at[k, j, bottom], t1.at[1], m1(-1))
            elif b == 1:
                ind2[p, 1] = put(buf.at[k, j, bottom], t2.at[0, bottom], m1(1))
            elif b == -1:
                ind2[p, -1] = put(buf.at[k, j, top], t2.at[1, top], m1(-1))
    zq[4, 1].wait_recv()
    zq[4, -1].wait_recv()
    add(cc.at[z], q4.at[0], q4.at[1])
    last = []
    for n, (dy, dx) in enumerate(plane):
        to = m4(y, dy) * 4 + m4(x, dx)
        last.append(put(cc.at[z, to], xcr.at[n], dev(dy, dx)))
    for p, (buf, r1, r2, t1, t2, zr, k, i, part, size, m2, m1, where) in enumerate(sums):
        st2[p, 1].wait_recv()
        add(buf.at[k, m4(i, 1), top], t1.at[0])
        dep2[p, 1] = put(buf.at[k, m4(i, 1), top], t2.at[0, top], m1(1))
        st2[p, -1].wait_recv()
        add(buf.at[k, m4(i, -1), bottom], t1.at[1])
        dep2[p, -1] = put(buf.at[k, m4(i, -1), bottom], t2.at[1, bottom], m1(-1))
    for p, (buf, r1, r2, t1, t2, zr, k, i, part, size, m2, m1, where) in enumerate(sums):
        for d in (1, -1):
            ind2[p, d].wait_recv()
            dep2[p, d].wait_recv()
        add(buf.at[k, i], t2.at[0], t2.at[1])
        for d in range(1, 8):
            last.append(put(buf.at[k, i, :, lanes(m8(z, d) * size, size)], zr.at[d - 1], dev(dz=d)))
    for copy in last:
        copy.wait_recv()
    fa = ca[ka, kb, :, lanes(z * NA, NA)].astype(F32)
    fb = cb[kb, ka, :, lanes(z * NB, NB)].astype(F32)
    for d in range(7):
        fa += za[d].astype(F32)
        fb += zb[d].astype(F32)
    fc = cc[z, g].astype(F32)
    for n in range(15):
        fc += xcr[n].astype(F32)
    mixed = fc[:, 128:]
    turned = pltpu.roll(mixed, 64, 1)
    upper = jnp.concatenate([fb, fc[:, :128]], axis=1)

    @pl.when(c == 0)
    def _():
        out[0:32, :] = jnp.concatenate([fa, mixed], axis=1)[:, :448].astype(BF16)
        out[32:64, :] = jnp.concatenate([upper, turned], axis=1)[:, :448].astype(BF16)

    @pl.when(c == 1)
    def _():
        out[0:32, :] = pltpu.roll(jnp.concatenate([mixed, fa], axis=1), 448, 1)[:, :448].astype(BF16)
        out[32:64, :] = pltpu.roll(jnp.concatenate([turned, upper], axis=1), 448, 1)[:, :448].astype(BF16)

    for copy in started:
        copy.wait_send()


def local(tokens, gate_scores, expert_ids, gate_weight, up_weight, down_weight):
    vmem = pl.BlockSpec(memory_space=pltpu.VMEM)
    anywhere = pl.BlockSpec(memory_space=pl.ANY)

    def route(size):
        width = 8 * size
        return [
            pltpu.VMEM((2, 4, 16, width), BF16), pltpu.VMEM((2, 4, 32, width), BF16),
            pltpu.VMEM((2, 16, width), BF16), pltpu.VMEM((2, 32, width), BF16),
            pltpu.VMEM((7, 32, size), BF16),
        ]

    return pl.pallas_call(
        kernel,
        out_shape=jax.ShapeDtypeStruct((64, 448), BF16),
        in_specs=[anywhere, vmem, vmem, anywhere, anywhere, anywhere],
        out_specs=vmem,
        scratch_shapes=[
            pltpu.VMEM((2, 4, 4, 64, PART), BF16),
            pltpu.VMEM((2, 4, 4, 64, PART), BF16),
            pltpu.VMEM((2, 8, 16, 64, 128), BF16),
            pltpu.VMEM((7168, 512), BF16),
            pltpu.VMEM((2, 256, 7168), BF16),
            pltpu.VMEM((16, 64, 512), F32),
            pltpu.VMEM((16, 8, 128), F32),
            pltpu.VMEM((16, 8, 128), F32),
            pltpu.VMEM((16, 64, 256), F32),
            pltpu.VMEM((2, 2, 16, 32, 256), BF16),
            pltpu.VMEM((4, 4, 32, 8 * NA), BF16),
            pltpu.VMEM((4, 4, 32, 8 * NB), BF16),
            pltpu.VMEM((8, 16, 32, 256), BF16),
            *route(NA),
            *route(NB),
            pltpu.VMEM((2, 8, 32, 256), BF16),
            pltpu.VMEM((2, 16, 32, 256), BF16),
            pltpu.VMEM((2, 16, 32, 256), BF16),
            pltpu.VMEM((2, 16, 32, 256), BF16),
            pltpu.VMEM((15, 32, 256), BF16),
            pltpu.SemaphoreType.DMA((COPIES,)),
            pltpu.SemaphoreType.DMA((COPIES,)),
            pltpu.SemaphoreType.DMA((9,)),
        ],
        compiler_params=pltpu.CompilerParams(
            collective_id=0, has_side_effects=True, vmem_limit_bytes=66 * 1024 * 1024 - 2 * 1024 * 1024 - 65536
        ),
    )(tokens, gate_scores, expert_ids, gate_weight, up_weight, down_weight)


def solution(mesh):
    torus = Mesh(mesh.devices.reshape(4, 4, 8, 2), ("y", "x", "z", "c"))
    return jax.shard_map(
        local,
        mesh=torus,
        in_specs=(
            P(("y", "x"), None),
            P(("y", "x"), None),
            P(("y", "x"), None),
            P(("y", "x"), None, ("z", "c")),
            P(("y", "x"), None, ("z", "c")),
            P(("y", "x"), ("z", "c"), None),
        ),
        out_specs=P(("y", "x"), ("z", "c")),
        check_vma=False,
    )
```

time: 364 us -> 102 us (0.28)
  blocking collectives: 130 us -> 0 us
  waiting for transfers between devices: 116 us -> 0 us
  Pallas kernels: 0 us -> 96.6 us
  local copies, waits for them, and re-layouts: 76.1 us -> 4.22 us
  matrix products: 18.5 us -> 0 us
  between operations: 13.5 us -> 0.01 us
  starting transfers between devices: 6.57 us -> 0 us
    all_to_all x1 -> x0, blocking collectives: 130 us -> none  [local(): lax.all_to_all(outgoing, 'ep', split_axis=0, concat_axis=0, tiled=True)]
    reduce_scatter x2 -> x0, waiting for transfers between devices: 107 us -> none  [sum_in_order(): tiles = lax.psum_scatter(tiles, axes[k], scatter_dimension=0, tiled=True)]
    pallas_call x0 -> x1, Pallas kernels: none -> 96.6 us  [local(): pl.pallas_call(kernel, out_shape=jax.ShapeDtypeStruct((64, 448), BF16), i...]
    reshape x2 -> x0, local copies, waits for them, and re-layouts: 41 us -> none  [the longest x1 21.7 us: in_blocks(): array.reshape(*lengths[:dim], size, lengths[dim] // size, *lengths[dim +...]
    dot_general x3 -> x0, matrix products: 18.5 us -> none  [the longest x1 13.2 us: local(): jnp.einsum('sjcf,jfd->sjcd', hidden, down_weight, preferred_element_type=...]
    gather x7 -> x0, local copies, waits for them, and re-layouts: 15.5 us -> none  [the longest x1 9.47 us: local(): outgoing = padded[index].reshape(n_ep, exp_local, capacity, width)]
    transpose x1 -> x0, local copies, waits for them, and re-layouts: 13 us -> none  [sum_in_order(): tiles = jnp.moveaxis(tiles, turns, range(len(axes))).reshape(-1, *inside)]
    all_to_all x1 -> x0, waiting for transfers between devices: 8.68 us -> none  [local(): lax.all_to_all(summed, 'ep', split_axis=0, concat_axis=0, tiled=True)]
  transfers between devices with their start and end apart: 3 -> 0, of which waited for: 3 -> 0; matrix products, arithmetic and copies ran while one was open for 1% -> 0% of each run, Pallas kernels for 0% -> 0%
where the time goes in v1:
time: 102 us; the launch traced here: 101 us
  Pallas kernels  96.6 us (95%)
  local copies, waits for them, and re-layouts  4.22 us (4%)
    pallas_call x1, Pallas kernels, local(): pl.pallas_call(kernel, out_shape=jax.ShapeDtypeStruct((64, 448), BF16), i...  96.6 us
    unnamed x3, local copies, waits for them, and re-layouts  4.22 us

profile of v1, /device:TPU:1, one launch (start us, length us, event | category | flops | bytes accessed | tf_op | source)
XLA Modules:
  0.0 100.8 jit_solution(14695353147435722349)
XLA Ops:
  0.0 1.4 %copy.7.score = f32[64,8]{1,0:T(8,128)} copy(f32[64,8]{0,1:T(8,128)} %param.7) | data formatting | bytes 4096 | tf_op args[1]
  1.4 1.4 %copy.8.ids = s32[64,8]{1,0:T(8,128)} copy(s32[64,8]{0,1:T(8,128)} %param.8) | data formatting | bytes 4096 | tf_op args[2]
  2.8 96.6 %shard_map.64 = bf16[64,448]{1,0:T(8,128)(2,1)} custom-call(bf16[64,7168]{1,0:T(8,128)(2,1)} %tok.1, f32[64,8]{1,0:T(8,128)} %copy.7.score, s32[64,8]{1,0:T(8,128)} %copy.8.ids, bf16[2,7168,128]{2,1,0:T(8,128)(2,1)} %gate_w.1, bf16[2,7168,128]{2,1,0:T(8,128)(2,1)} %up_w.1, bf16[2,128,7168]{2,1,0:T(8,128)(2,1)} %down_w.1), custom_call_target="tpu_custom_call" | custom-call | tf_op jit(solution)/shard_map/pallas_call | solution.py:429
  99.4 1.5 %copy.10 = bf16[64,448]{1,0:T(8,128)(2,1)} copy(bf16[64,448]{1,0:T(8,128)(2,1)} %shard_map.64) | data formatting | bytes 114688

commit v2 on v0

v2 whole, which is shorter than its diff:
```python
import jax
import jax.numpy as jnp
from jax import lax
from jax.experimental import pallas as pl
from jax.experimental.pallas import tpu as pltpu
from jax.sharding import Mesh
from jax.sharding import PartitionSpec as P

F32, BF16 = jnp.float32, jnp.bfloat16
HALF = 3584
PART = 1280
ZOFF = 2 * PART
WIDTHS = (384, 256)
CHUNKS = 2
TH = 64 // CHUNKS
RH = TH // 2
ROWS = ((0,), (-1, 1), (2,), (0, -1, 1), (0, -1, 1, 2))
PIECES = ((0, -1, 1, -2), (2, -3, 3, 4), (0, -1, 1, -2, 2, -3, 3, 4))
SENDS, RECVS = 25 * CHUNKS + 2, 59 * CHUNKS + 2


def kernel(
    tok, score, ids, gate_w, up_w, down_w, out,
    xa, xb, xc, wgu, wd, acc, wsend, wrecv, wcol, hid,
    ca, cb, cc, r1a, r2a, t1a, t2a, za, r1b, r2b, t1b, t2b, zb, q1, q2, q3, q4, xcr,
    send, recv, loc,
):
    y, x = lax.axis_index("y"), lax.axis_index("x")
    z, c = lax.axis_index("z"), lax.axis_index("c")
    g = y * 4 + x
    oc = 1 - c

    def m4(v, d):
        return lax.rem(v + (4 + d), 4)

    def m8(v, d):
        return lax.rem(v + (8 + d), 8)

    def dev(dy=0, dx=0, dz=0):
        return (m4(y, dy), m4(x, dx), m8(z, dz), c)

    sibling = (y, x, z, oc)
    counts = {"send": 0, "recv": 0}
    send_waits = []

    class Batch:
        def __init__(self, kind, ref):
            self.sem = (send if kind == "send" else recv).at[counts[kind]]
            self.ref = ref
            counts[kind] += 1
            assert counts[kind] <= (SENDS if kind == "send" else RECVS)
            if kind == "send":
                send_waits.append(self)

        def wait(self):
            pltpu.make_async_copy(self.ref, self.ref, self.sem).wait()

    def sends(ref):
        return Batch("send", ref)

    def recvs(ref):
        return Batch("recv", ref)

    def put(src, dst, device, out_batch, in_batch):
        pltpu.make_async_remote_copy(
            src_ref=src, dst_ref=dst, send_sem=out_batch.sem, recv_sem=in_batch.sem,
            device_id=device, device_id_type=pl.DeviceIdType.MESH,
        ).start()

    def lanes(start, size):
        return pl.ds(pl.multiple_of(start, 128), size)

    def mark(*_):
        pass

    plane = [(dy, dx) for dy in range(4) for dx in range(4) if dy or dx]
    everyone = range(CHUNKS)

    mark("a00_start")
    own = []
    for h in everyone:
        rows = pl.ds(h * TH, TH)
        own += [
            pltpu.make_async_copy(tok.at[rows, lanes(c * HALF + ZOFF + z * 128, 128)], xc.at[h, c, z, g], loc.at[3 * h]),
            pltpu.make_async_copy(tok.at[rows, lanes(c * HALF, PART)], xa.at[h, c, y * 4 + x], loc.at[3 * h + 1]),
            pltpu.make_async_copy(tok.at[rows, lanes(c * HALF + PART, PART)], xb.at[h, c, x * 4 + y], loc.at[3 * h + 2]),
        ]
    for copy in own:
        copy.start()
    barrier = pltpu.get_barrier_semaphore()
    for dy, dx in plane:
        pl.semaphore_signal(barrier, inc=1, device_id=dev(dy, dx), device_id_type=pl.DeviceIdType.MESH)
    for d in range(1, 8):
        pl.semaphore_signal(barrier, inc=1, device_id=dev(dz=d), device_id_type=pl.DeviceIdType.MESH)
    pl.semaphore_signal(barrier, inc=1, device_id=sibling, device_id_type=pl.DeviceIdType.MESH)
    for copy in own:
        copy.wait()
    loads = []
    wsem, dsem = loc.at[3 * CHUNKS], loc.at[3 * CHUNKS + 1]
    for e in range(2):
        pltpu.make_async_copy(gate_w.at[e], wgu.at[:, pl.ds(e * 256, 128)], wsem).start()
        pltpu.make_async_copy(up_w.at[e], wgu.at[:, pl.ds(e * 256 + 128, 128)], wsem).start()
    for e in range(2):
        pltpu.make_async_copy(down_w.at[e], wd.at[c, pl.ds(e * 128, 128)], dsem).start()
    mark("a01_barrier")
    pl.semaphore_wait(barrier, 23)

    w_out, w_in = sends(wsend.at[pl.ds(0, 15)]), recvs(wrecv.at[pl.ds(0, 15)])
    down_out, down_in = sends(wd.at[c]), recvs(wd.at[oc])

    def routing():
        line = lax.broadcasted_iota(jnp.int32, (128, 64), 0)
        expert = jnp.where((line & 7) < 2, (line >> 3) * 2 + (line & 7), -1)
        s = score[...]
        norm = 2.5 * s / jnp.sum(s, axis=0, keepdims=True)
        dense = jnp.zeros((128, 64), F32)
        for t in range(8):
            dense += jnp.where(ids[t : t + 1, :] == expert, norm[t : t + 1, :], 0.0)
        wsend[...] = jnp.zeros_like(wsend)
        wsend[:, :, 0:64] = dense.reshape(16, 8, 64)
        acc[...] = jnp.zeros_like(acc)
        wrecv[g] = wsend[g]
        for dy, dx in plane:
            put(wsend.at[m4(y, dy) * 4 + m4(x, dx)], wrecv.at[g], dev(dy, dx), w_out, w_in)
        for e in range(2):
            put(down_w.at[e], wd.at[c, pl.ds(e * 128, 128)], sibling, down_out, down_in)

    def routing_done():
        w_in.wait()
        wt = wrecv[...].reshape(128, 128).T
        lane = lax.broadcasted_iota(jnp.int32, (64, 128), 1)

        @pl.loop(0, 16)
        def _(q):
            for e in range(2):
                col = jnp.sum(jnp.where(lane == q * 8 + e, wt[:64], 0.0), axis=1, keepdims=True)
                wcol[q, :, e * 128 : (e + 1) * 128] = jnp.broadcast_to(col, (64, 128))

    class Gather:
        def __init__(self, h):
            self.h = h
            self.routes = (
                (xa.at[h], y, x, lambda d: dev(dx=d), lambda d: dev(dy=d), 0, lambda k, j: k * 4 + j),
                (xb.at[h], x, y, lambda d: dev(dy=d), lambda d: dev(dx=d), PART, lambda k, j: j * 4 + k),
            )
            self.xc = xc.at[h]
            two = [buf.at[c, pl.ds(0, 2)] for buf in (xa.at[h], xb.at[h])]
            self.block_out = [sends(buf.at[c, pl.ds(0, 15)]) for buf in (xa.at[h], xb.at[h])]
            self.row_out = [sends(buf.at[c]) for buf in (xa.at[h], xb.at[h])]
            self.piece_out = sends(xc.at[h, c, z, pl.ds(0, 15)])
            self.z_out = sends(xc.at[h, c, pl.ds(0, 7)])
            self.zsib_out = sends(xc.at[h, c])
            self.piece_in = recvs(xc.at[h, c, z, pl.ds(0, 15)])
            self.first_in = [recvs(ref) for ref in two]
            self.half1_in = [recvs(buf.at[c, 0]) for buf in (xa.at[h], xb.at[h])]
            self.full2_in = {(p, b): recvs(two[p]) for p in range(2) for b in (0, -1, 1, 2)}
            self.half2_in = [recvs(buf.at[c, pl.ds(0, 4)]) for buf in (xa.at[h], xb.at[h])]
            self.z_in = {(t, d): recvs(xc.at[h, c, 0] if t < 3 else xc.at[h, c, 0, pl.ds(0, 8)]) for t in range(4) for d in (1, -1)}
            self.row_in = {(p, n): recvs(buf.at[c, pl.ds(0, 8 if n == 1 else 4)]) for p, buf in enumerate((xa.at[h], xb.at[h])) for n in range(3)}
            self.zsib_in = [recvs(xc.at[h, c, pl.ds(0, n)]) for n in (4, 4)]

        def begin_pieces(self):
            for s in plane:
                ref = self.xc.at[c, z, g]
                put(ref, ref, dev(*s), self.piece_out, self.piece_in)

        def begin_first(self):
            for p, (buf, k, i, m1, m2, off, rows) in enumerate(self.routes):
                for d in (1, -1):
                    ref = buf.at[c, k * 4 + i]
                    put(ref, ref, m1(d), self.block_out[p], self.first_in[p])

        def begin_second(self):
            for p, (buf, k, i, m1, m2, off, rows) in enumerate(self.routes):
                for d in (1, -1):
                    ref = buf.at[c, k * 4 + i]
                    put(ref, ref, m2(d), self.block_out[p], self.full2_in[p, 0])

        def z_sib(self, zz, n):
            put(self.xc.at[c, zz], self.xc.at[c, zz], sibling, self.zsib_out, self.zsib_in[n])

        def pieces(self):
            self.piece_in.wait()
            ref = self.xc.at[c, z]
            for d in (1, -1):
                put(ref, ref, dev(dz=d), self.z_out, self.z_in[0, d])
            self.z_sib(z, 0)

        def firsts(self):
            for p, (buf, k, i, m1, m2, off, rows) in enumerate(self.routes):
                self.first_in[p].wait()
                ref = buf.at[c, k * 4 + m4(i, -1), pl.ds(0, RH)]
                put(ref, ref, m1(1), self.block_out[p], self.half1_in[p])
                ref = buf.at[c, k * 4 + m4(i, 1), pl.ds(RH, RH)]
                put(ref, ref, m1(-1), self.block_out[p], self.half1_in[p])
            for b in (-1, 1):
                for p in range(2):
                    self.forward(p, b)

        def forward(self, p, b):
            buf, k, i, m1, m2, off, rows = self.routes[p]
            ref = buf.at[c, k * 4 + m4(i, b)]
            for d in (1, -1):
                put(ref, ref, m2(d), self.block_out[p], self.full2_in[p, b])

        def row_sib(self, p, b, batch):
            buf, k = self.routes[p][:2]
            ref = buf.at[c, pl.ds(m4(k, b) * 4, 4)]
            put(ref, ref, sibling, self.row_out[p], batch)

        def halves(self):
            for p in range(2):
                self.half1_in[p].wait()
                self.forward(p, 2)
            for p in range(2):
                self.row_sib(p, 0, self.row_in[p, 0])

        def pass_on(self, b):
            for p, (buf, k, i, m1, m2, off, rows) in enumerate(self.routes):
                self.full2_in[p, b].wait()
                ref = buf.at[c, m4(k, -1) * 4 + m4(i, b), pl.ds(0, RH)]
                put(ref, ref, m2(1), self.block_out[p], self.half2_in[p])
                ref = buf.at[c, m4(k, 1) * 4 + m4(i, b), pl.ds(RH, RH)]
                put(ref, ref, m2(-1), self.block_out[p], self.half2_in[p])
                if b == 2:
                    self.row_sib(p, -1, self.row_in[p, 1])
                    self.row_sib(p, 1, self.row_in[p, 1])

        def z_step(self, t):
            for d in (1, -1):
                self.z_in[t - 1, d].wait()
                zz = m8(z, -d * t)
                if t < 3:
                    put(self.xc.at[c, zz], self.xc.at[c, zz], dev(dz=d), self.z_out, self.z_in[t, d])
                elif t == 3:
                    part = pl.ds(0 if d == 1 else 8, 8)
                    put(self.xc.at[c, zz, part], self.xc.at[c, zz, part], dev(dz=d), self.z_out, self.z_in[t, d])
                if t < 4:
                    self.z_sib(zz, {(1, 1): 0, (1, -1): 0, (2, 1): 0, (2, -1): 1, (3, 1): 1, (3, -1): 1}[t, d])
            if t == 4:
                self.z_sib(m8(z, 4), 1)

        def mul(self, p, src, part):
            buf, k, i, m1, m2, off, rows = self.routes[p]
            start = pl.multiple_of(src * HALF + off, 128)
            ks = [m4(k, b) for b in ROWS[part]]
            m = 4 * TH
            left = jnp.concatenate([buf[src, pl.ds(kk * 4, 4)].reshape(m, PART) for kk in ks], axis=0)

            @pl.loop(0, 2)
            def _(n):
                cols = lanes(n * 256, 256)
                r = jnp.dot(left, wgu[pl.ds(start, PART), cols], preferred_element_type=F32)
                for a, kk in enumerate(ks):
                    for j in range(4):
                        low = a * m + j * TH
                        acc[rows(kk, j), pl.ds(self.h * TH, TH), cols] += r[low : low + TH]

        def mulz(self, src, n):
            zs = [m8(z, b) for b in PIECES[n]]
            starts = [pl.multiple_of(src * HALF + ZOFF + zz * 128, 128) for zz in zs]
            per = 256 // TH

            @pl.loop(0, 16 // per)
            def _(q):
                some = pl.ds(q * per, per)
                left = jnp.concatenate([self.xc[src, zz, some].reshape(256, 128) for zz in zs], axis=1)
                right = jnp.concatenate([wgu[pl.ds(s, 128), :] for s in starts], axis=0)
                r = jnp.dot(left, right, preferred_element_type=F32)
                acc[some, pl.ds(self.h * TH, TH), :] += r.reshape(per, TH, 512)

        def late(self):
            for p in range(2):
                self.half2_in[p].wait()
                self.row_sib(p, 2, self.row_in[p, 2])

        def own_rows(self, n):
            for p in range(2):
                self.mul(p, c, n)

        def sib_rows(self, n):
            for p in range(2):
                for batch in ((0,), (1,), (2,), (0, 1), (0, 1, 2))[n]:
                    self.row_in[p, batch].wait()
                self.mul(p, oc, n)

        def sib_z(self, n):
            for batch in ((0,), (1,), (0, 1))[n]:
                self.zsib_in[batch].wait()
            self.mulz(oc, n)

        def hidden(self):
            h = self.h
            rows = pl.ds(h * TH, TH)

            @pl.loop(0, 16)
            def _(q):
                for e in range(2):
                    gate = acc[q, rows, e * 256 : e * 256 + 128]
                    upper = acc[q, rows, e * 256 + 128 : e * 256 + 256]
                    value = gate / (1.0 + jnp.exp(-gate)) * upper * wcol[q, rows, e * 128 : (e + 1) * 128]
                    value = value.astype(BF16)
                    hid[h, c, 0, q, :, e * 128 : (e + 1) * 128] = value[:RH]
                    hid[h, c, 1, q, :, e * 128 : (e + 1) * 128] = value[RH:]

            self.hid_in = recvs(hid.at[h, c])
            put(hid.at[h, c], hid.at[h, c], sibling, sends(hid.at[h, c]), self.hid_in)

    ka, kb = y * oc + x * c, x * oc + y * c

    def along(other, d):
        u, v = d * c, d * oc
        if other:
            return (lax.rem(y + 4 + u, 4), lax.rem(x + 4 + v, 4), z, c)
        return (lax.rem(y + 4 + v, 4), lax.rem(x + 4 + u, 4), z, c)

    def down(left, right, start, size):
        return jnp.dot(left, wd[0, :, lanes(start, size)], preferred_element_type=F32) + jnp.dot(
            right, wd[1, :, lanes(start, size)], preferred_element_type=F32
        )

    def add(*refs):
        total = refs[0][...].astype(F32)
        for ref in refs[1:]:
            total += ref[...].astype(F32)
        refs[0][...] = total.astype(BF16)

    order = (2, 1, -1, 0)
    side = (lax.broadcasted_iota(jnp.int32, (16 * RH, 128), 1) < 64) == (c == 0)

    class Sum:
        def __init__(self, h):
            self.h = h
            self.routes = (
                (ca.at[h], r1a.at[h], r2a.at[h], t1a.at[h], t2a.at[h], za.at[h], ka, kb, WIDTHS[0],
                 lambda d: along(False, d), lambda d: along(True, d)),
                (cb.at[h], r1b.at[h], r2b.at[h], t1b.at[h], t2b.at[h], zb.at[h], kb, ka, WIDTHS[1],
                 lambda d: along(True, d), lambda d: along(False, d)),
            )
            self.hid = hid.at[h]
            self.cc, self.q = cc.at[h], [None, q1.at[h], q2.at[h], q3.at[h], q4.at[h]]
            self.st1 = [(sends(r[1]), recvs(r[1])) for r in self.routes]
            self.ind = [(sends(r[2].at[0]), recvs(r[2].at[0])) for r in self.routes]
            self.dep_out = [sends(r[2].at[0]) for r in self.routes]
            self.dep_in = {(p, b): recvs(self.routes[p][2].at[0, 0]) for p in range(2) for b in order}
            self.st2 = [(sends(r[3]), recvs(r[3])) for r in self.routes]
            self.t2 = [(sends(r[4]), recvs(r[4])) for r in self.routes]
            self.zr = [(sends(r[5]), recvs(r[5])) for r in self.routes]
            self.q_out = [None] + [sends(q) for q in self.q[1:]]
            self.q_in = [None] + [(recvs(q.at[0]), recvs(q.at[1])) for q in self.q[1:]]
            self.xy = (sends(xcr.at[h]), recvs(xcr.at[h]))

        def cut(self, p):
            half = self.routes[p][8] * 4
            return pl.ds(0, half), pl.ds(half, half)

        def product(self, p):
            buf, size = self.routes[p][0], self.routes[p][8]
            left = self.hid[0, p].reshape(16 * RH, 256)
            right = self.hid[1, p].reshape(16 * RH, 256)
            for zz in range(8):
                r = down(left, right, zz * 896 + c * 512, size).astype(BF16)
                for q in range(16):
                    a, b = q // 4, q % 4
                    k, i = (a * oc + b * c, b * oc + a * c) if p == 0 else (b * oc + a * c, a * oc + b * c)
                    buf[k, i, :, zz * size : (zz + 1) * size] = r[q * RH : (q + 1) * RH]

        def begin(self, p):
            buf, r1, r2, t1, t2, zr, k, i, size, m2, m1 = self.routes[p]
            left, right = self.cut(p)
            self.product(p)
            put(buf.at[m4(k, 2), :, :, left], r1.at[0], m2(1), *self.st1[p])
            put(buf.at[m4(k, 2), :, :, right], r1.at[1], m2(-1), *self.st1[p])

        def independent(self, p):
            buf, r1, r2, t1, t2, zr, k, i, size, m2, m1 = self.routes[p]
            left, right = self.cut(p)
            put(buf.at[m4(k, 1), :, :, right], r2.at[0, :, :, right], m2(1), *self.ind[p])
            put(buf.at[m4(k, -1), :, :, left], r2.at[1, :, :, left], m2(-1), *self.ind[p])

        def columns(self, zs):
            lo = [self.hid[n, 0].reshape(16 * RH, 256) for n in range(2)]
            hi = [self.hid[n, 1].reshape(16 * RH, 256) for n in range(2)]

            def weights(*starts):
                return [jnp.concatenate([wd[n, :, lanes(s, 128)] for s in starts], axis=1) for n in range(2)]

            def dot(left, right):
                return jnp.dot(left[0], right[0], preferred_element_type=F32) + jnp.dot(left[1], right[1], preferred_element_type=F32)

            r_lo = dot(lo, weights(*(zz * 896 + 384 for zz in zs)))
            for n, zz in enumerate(zs):
                r = dot(hi, weights(zz * 896 + c * 512 + 256, zz * 896 + 384))
                self.cc[zz, :, :, 0:128] = r[:, :128].reshape(16, RH, 128).astype(BF16)
                r = jnp.where(side, r_lo[:, n * 128 : (n + 1) * 128], pltpu.roll(r[:, 128:], 64, 1))
                self.cc[zz, :, :, 128:256] = r.reshape(16, RH, 128).astype(BF16)

        def first_columns(self):
            first, second = pl.ds(0, 8), pl.ds(8, 8)
            cc_, q = self.cc, self.q
            self.columns((m8(z, 4), m8(z, 3)))
            put(cc_.at[m8(z, 4), first], q[1].at[0], dev(dz=1), self.q_out[1], self.q_in[1][0])
            put(cc_.at[m8(z, 4), second], q[1].at[1], dev(dz=-1), self.q_out[1], self.q_in[1][1])
            put(cc_.at[m8(z, 3), second], q[2].at[0, second], dev(dz=1), self.q_out[2], self.q_in[2][0])
            self.columns((m8(z, -3), m8(z, 2)))
            put(cc_.at[m8(z, -3), first], q[2].at[1, first], dev(dz=-1), self.q_out[2], self.q_in[2][1])

        def last_columns(self):
            self.columns((m8(z, -2), m8(z, 1)))
            self.columns((m8(z, -1), z))

        def z_second(self):
            first, second = pl.ds(0, 8), pl.ds(8, 8)
            cc_, q = self.cc, self.q
            self.q_in[1][0].wait()
            add(cc_.at[m8(z, 3), first], q[1].at[0])
            put(cc_.at[m8(z, 3), first], q[2].at[0, first], dev(dz=1), self.q_out[2], self.q_in[2][0])
            self.q_in[1][1].wait()
            add(cc_.at[m8(z, -3), second], q[1].at[1])
            put(cc_.at[m8(z, -3), second], q[2].at[1, second], dev(dz=-1), self.q_out[2], self.q_in[2][1])

        def z_next(self, t):
            for n, d in enumerate((1, -1)):
                self.q_in[t][n].wait()
                ref = self.cc.at[m8(z, d * (4 - t))]
                add(ref, self.q[t].at[n])
                put(ref, self.q[t + 1].at[n], dev(dz=d), self.q_out[t + 1], self.q_in[t + 1][n])

        def z_end(self):
            self.q_in[4][0].wait()
            self.q_in[4][1].wait()
            add(self.cc.at[z], self.q[4].at[0], self.q[4].at[1])
            for n, (dy, dx) in enumerate(plane):
                to = m4(y, dy) * 4 + m4(x, dx)
                put(self.cc.at[z, to], xcr.at[self.h, n], dev(dy, dx), *self.xy)

        def depend(self, p):
            buf, r1, r2, t1, t2, zr, k, i, size, m2, m1 = self.routes[p]
            left, right = self.cut(p)
            self.st1[p][1].wait()
            for b in order:
                j = m4(i, b)
                ref = buf.at[m4(k, 1), j, :, left]
                add(ref, r1.at[0, j])
                put(ref, r2.at[0, j, :, left], m2(1), self.dep_out[p], self.dep_in[p, b])
                ref = buf.at[m4(k, -1), j, :, right]
                add(ref, r1.at[1, j])
                put(ref, r2.at[1, j, :, right], m2(-1), self.dep_out[p], self.dep_in[p, b])

        def second(self, *blocks):
            for b in blocks:
                for p, (buf, r1, r2, t1, t2, zr, k, i, size, m2, m1) in enumerate(self.routes):
                    left, right = self.cut(p)
                    if b == 2:
                        self.ind[p][1].wait()
                    self.dep_in[p, b].wait()
                    j = m4(i, b)
                    add(buf.at[k, j], r2.at[0, j], r2.at[1, j])
                    if b == 2:
                        put(buf.at[k, j, :, left], t1.at[0], m1(1), *self.st2[p])
                        put(buf.at[k, j, :, right], t1.at[1], m1(-1), *self.st2[p])
                    elif b == 1:
                        put(buf.at[k, j, :, right], t2.at[0, :, right], m1(1), *self.t2[p])
                    elif b == -1:
                        put(buf.at[k, j, :, left], t2.at[1, :, left], m1(-1), *self.t2[p])

        def third(self):
            for p, (buf, r1, r2, t1, t2, zr, k, i, size, m2, m1) in enumerate(self.routes):
                left, right = self.cut(p)
                self.st2[p][1].wait()
                ref = buf.at[k, m4(i, 1), :, left]
                add(ref, t1.at[0])
                put(ref, t2.at[0, :, left], m1(1), *self.t2[p])
                ref = buf.at[k, m4(i, -1), :, right]
                add(ref, t1.at[1])
                put(ref, t2.at[1, :, right], m1(-1), *self.t2[p])

        def fourth(self):
            for p, (buf, r1, r2, t1, t2, zr, k, i, size, m2, m1) in enumerate(self.routes):
                self.t2[p][1].wait()
                add(buf.at[k, i], t2.at[0], t2.at[1])
                for d in (4, 3, -3, 2, -2, 1, -1):
                    n = d - 1 if d > 0 else d + 7
                    put(buf.at[k, i, :, lanes(m8(z, d) * size, size)], zr.at[n], dev(dz=d), *self.zr[p])

        def finish(self):
            h = self.h
            self.xy[1].wait()
            fc = self.cc[z, g].astype(F32)
            for n in range(15):
                fc += xcr[h, n].astype(F32)
            total = []
            for p, (buf, r1, r2, t1, t2, zr, k, i, size, m2, m1) in enumerate(self.routes):
                self.zr[p][1].wait()
                f = buf[k, i, :, lanes(z * size, size)].astype(F32)
                for d in range(7):
                    f += zr[d].astype(F32)
                total.append(f)
            fa, fb = total
            mixed = fc[:, 128:]
            turned = pltpu.roll(mixed, 64, 1)
            upper = jnp.concatenate([fb, fc[:, :128]], axis=1)
            one, two = slice(h * TH, h * TH + RH), slice(h * TH + RH, (h + 1) * TH)

            @pl.when(c == 0)
            def _():
                out[one, :] = jnp.concatenate([fa, mixed], axis=1)[:, :448].astype(BF16)
                out[two, :] = jnp.concatenate([upper, turned], axis=1)[:, :448].astype(BF16)

            @pl.when(c == 1)
            def _():
                out[one, :] = pltpu.roll(jnp.concatenate([mixed, fa], axis=1), 448, 1)[:, :448].astype(BF16)
                out[two, :] = pltpu.roll(jnp.concatenate([turned, upper], axis=1), 448, 1)[:, :448].astype(BF16)

    G = [Gather(h) for h in everyone]
    S = [Sum(h) for h in everyone]
    loads_in = [pltpu.make_async_copy(wgu, wgu, wsem), pltpu.make_async_copy(wd.at[c], wd.at[c], dsem)]

    def run(*steps):
        for n, step in enumerate(steps):
            call, rest = (step[0], step[1:]) if isinstance(step, tuple) else (step, ())
            mark(n, call, rest)
            call(*rest)

    def exchanged(h):
        G[h].hid_in.wait()

    a, b = G
    s, t = S
    run(
        a.begin_pieces, a.begin_first, a.begin_second, routing,
        a.pieces, a.firsts, b.begin_pieces, loads_in[0].wait, loads_in[1].wait,
        a.halves, (a.pass_on, 0), b.begin_first, (a.z_step, 1), (a.own_rows, 0),
        (a.pass_on, -1), routing_done, (a.pass_on, 1), b.begin_second, (a.sib_rows, 0), (a.z_step, 2), (a.pass_on, 2),
        b.pieces, (a.own_rows, 1), (a.mulz, c, 0), b.firsts, (a.sib_z, 0), (a.sib_rows, 1), (a.z_step, 3),
        a.late, (a.own_rows, 2), (b.z_step, 1), b.halves, (b.pass_on, 0), (a.z_step, 4), (a.mulz, c, 1),
        (b.pass_on, -1), (a.sib_rows, 2), (b.pass_on, 1), (a.sib_z, 1), a.hidden,
        (b.z_step, 2), (b.pass_on, 2), (b.own_rows, 3), down_in.wait, (exchanged, 0),
        s.first_columns, (s.begin, 0), (s.begin, 1), (s.independent, 0), (s.independent, 1), (b.z_step, 3), b.late,
        (b.mulz, c, 0), (b.sib_rows, 3), s.z_second, (b.own_rows, 2), s.last_columns, (b.z_step, 4),
        (b.mulz, c, 1), (b.sib_rows, 2), (s.depend, 0), (s.depend, 1), (s.z_next, 2), (b.sib_z, 2), b.hidden,
        (exchanged, 1), t.first_columns, (s.second, 2), (t.begin, 0), (s.second, 1, -1, 0), (t.begin, 1),
        (t.independent, 0), (t.independent, 1), t.last_columns, (s.z_next, 3), t.z_second, s.third, (t.depend, 0), (t.depend, 1),
        s.z_end, s.fourth, (t.z_next, 2), (t.second, 2), (t.second, 1), (t.z_next, 3), (t.second, -1, 0), t.third, t.z_end,
        t.fourth, s.finish, t.finish,
    )
    mark("b30_sends")
    for batch in send_waits:
        batch.wait()
    mark(None)


def local(tokens, gate_scores, expert_ids, gate_weight, up_weight, down_weight):
    vmem = pl.BlockSpec(memory_space=pltpu.VMEM)
    anywhere = pl.BlockSpec(memory_space=pl.ANY)

    def bf16(*shape):
        return pltpu.VMEM((CHUNKS, *shape), BF16)

    def route(size):
        w = 8 * size
        return [bf16(2, 4, RH, w // 2), bf16(2, 4, RH, w), bf16(2, RH, w // 2), bf16(2, RH, w), bf16(7, RH, size)]

    return pl.pallas_call(
        kernel,
        out_shape=jax.ShapeDtypeStruct((64, 448), BF16),
        in_specs=[anywhere, vmem, vmem, anywhere, anywhere, anywhere],
        out_specs=vmem,
        scratch_shapes=[
            bf16(2, 16, TH, PART),
            bf16(2, 16, TH, PART),
            bf16(2, 8, 16, TH, 128),
            pltpu.VMEM((7168, 512), BF16),
            pltpu.VMEM((2, 256, 7168), BF16),
            pltpu.VMEM((16, 64, 512), F32),
            pltpu.VMEM((16, 8, 128), F32),
            pltpu.VMEM((16, 8, 128), F32),
            pltpu.VMEM((16, 64, 256), F32),
            bf16(2, 2, 16, RH, 256),
            bf16(4, 4, RH, 8 * WIDTHS[0]),
            bf16(4, 4, RH, 8 * WIDTHS[1]),
            bf16(8, 16, RH, 256),
            *route(WIDTHS[0]),
            *route(WIDTHS[1]),
            bf16(2, 8, RH, 256),
            bf16(2, 16, RH, 256),
            bf16(2, 16, RH, 256),
            bf16(2, 16, RH, 256),
            bf16(15, RH, 256),
            pltpu.SemaphoreType.DMA((SENDS,)),
            pltpu.SemaphoreType.DMA((RECVS,)),
            pltpu.SemaphoreType.DMA((3 * CHUNKS + 2,)),
        ],
        compiler_params=pltpu.CompilerParams(
            collective_id=0, has_side_effects=True, vmem_limit_bytes=67043328
        ),
    )(tokens, gate_scores.T, expert_ids.T, gate_weight, up_weight, down_weight)


def solution(mesh):
    torus = Mesh(mesh.devices.reshape(4, 4, 8, 2), ("y", "x", "z", "c"))
    return jax.shard_map(
        local,
        mesh=torus,
        in_specs=(
            P(("y", "x"), None),
            P(("y", "x"), None),
            P(("y", "x"), None),
            P(("y", "x"), None, ("z", "c")),
            P(("y", "x"), None, ("z", "c")),
            P(("y", "x"), ("z", "c"), None),
        ),
        out_specs=P(("y", "x"), ("z", "c")),
        check_vma=False,
    )
```

time: 364 us -> 91 us (0.25)
  blocking collectives: 130 us -> 0 us
  waiting for transfers between devices: 116 us -> 0 us
  Pallas kernels: 0 us -> 89.3 us
  local copies, waits for them, and re-layouts: 76.1 us -> 1.47 us
  matrix products: 18.5 us -> 0 us
  between operations: 13.5 us -> 0.01 us
  starting transfers between devices: 6.57 us -> 0 us
    all_to_all x1 -> x0, blocking collectives: 130 us -> none  [local(): lax.all_to_all(outgoing, 'ep', split_axis=0, concat_axis=0, tiled=True)]
    reduce_scatter x2 -> x0, waiting for transfers between devices: 107 us -> none  [sum_in_order(): tiles = lax.psum_scatter(tiles, axes[k], scatter_dimension=0, tiled=True)]
    pallas_call x0 -> x1, Pallas kernels: none -> 89.3 us  [local(): pl.pallas_call(kernel, out_shape=jax.ShapeDtypeStruct((64, 448), BF16), i...]
    reshape x2 -> x0, local copies, waits for them, and re-layouts: 41 us -> none  [the longest x1 21.7 us: in_blocks(): array.reshape(*lengths[:dim], size, lengths[dim] // size, *lengths[dim +...]
    dot_general x3 -> x0, matrix products: 18.5 us -> none  [the longest x1 13.2 us: local(): jnp.einsum('sjcf,jfd->sjcd', hidden, down_weight, preferred_element_type=...]
    gather x7 -> x0, local copies, waits for them, and re-layouts: 15.5 us -> none  [the longest x1 9.47 us: local(): outgoing = padded[index].reshape(n_ep, exp_local, capacity, width)]
    transpose x1 -> x0, local copies, waits for them, and re-layouts: 13 us -> none  [sum_in_order(): tiles = jnp.moveaxis(tiles, turns, range(len(axes))).reshape(-1, *inside)]
    all_to_all x1 -> x0, waiting for transfers between devices: 8.68 us -> none  [local(): lax.all_to_all(summed, 'ep', split_axis=0, concat_axis=0, tiled=True)]
  transfers between devices with their start and end apart: 3 -> 0, of which waited for: 3 -> 0; matrix products, arithmetic and copies ran while one was open for 1% -> 0% of each run, Pallas kernels for 0% -> 0%
where the time goes in v2:
time: 91 us; the launch traced here: 90.8 us
  Pallas kernels  89.3 us (98%)
  local copies, waits for them, and re-layouts  1.47 us (2%)
    pallas_call x1, Pallas kernels, local(): pl.pallas_call(kernel, out_shape=jax.ShapeDtypeStruct((64, 448), BF16), i...  89.3 us

profile of v2, /device:TPU:1, one launch (start us, length us, event | category | flops | bytes accessed | tf_op | source)
XLA Modules:
  0.0 90.8 jit_solution(10561594171413484502)
XLA Ops:
  0.0 89.3 %shard_map.64 = bf16[64,448]{1,0:T(8,128)(2,1)} custom-call(bf16[64,7168]{1,0:T(8,128)(2,1)} %tok.1, f32[8,64]{1,0:T(8,128)} %bitcast.2, s32[8,64]{1,0:T(8,128)} %bitcast.3, bf16[2,7168,128]{2,1,0:T(8,128)(2,1)} %gate_w.1, bf16[2,7168,128]{2,1,0:T(8,128)(2,1)} %up_w.1, bf16[2,128,7168]{2,1,0:T(8,128)(2,1)} %down_w.1), custom_call_target="tpu_custom_call" | custom-call | tf_op jit(solution)/shard_map/pallas_call | solution.py:564
  89.3 1.5 %copy.8 = bf16[64,448]{1,0:T(8,128)(2,1)} copy(bf16[64,448]{1,0:T(8,128)(2,1)} %shard_map.64) | data formatting | bytes 114688

commit v3 on v2

--- a/solution.py
+++ b/solution.py
@@ -532,16 +532,16 @@
         a.pieces, a.firsts, b.begin_pieces, loads_in[0].wait, loads_in[1].wait,
         a.halves, (a.pass_on, 0), b.begin_first, (a.z_step, 1), (a.own_rows, 0),
         (a.pass_on, -1), routing_done, (a.pass_on, 1), b.begin_second, (a.sib_rows, 0), (a.z_step, 2), (a.pass_on, 2),
-        b.pieces, (a.own_rows, 1), (a.mulz, c, 0), b.firsts, (a.sib_z, 0), (a.sib_rows, 1), (a.z_step, 3),
-        a.late, (a.own_rows, 2), (b.z_step, 1), b.halves, (b.pass_on, 0), (a.z_step, 4), (a.mulz, c, 1),
-        (b.pass_on, -1), (a.sib_rows, 2), (b.pass_on, 1), (a.sib_z, 1), a.hidden,
-        (b.z_step, 2), (b.pass_on, 2), (b.own_rows, 3), down_in.wait, (exchanged, 0),
+        b.pieces, (a.own_rows, 1), (a.mulz, c, 0), (a.sib_z, 0), b.firsts, (a.z_step, 3), (a.sib_rows, 1),
+        a.late, (a.own_rows, 2), (b.z_step, 1), (a.z_step, 4), b.halves, (b.pass_on, 0), (a.mulz, c, 1),
+        (b.own_rows, 0), (b.pass_on, -1), (a.sib_rows, 2), (b.pass_on, 1), (a.sib_z, 1), a.hidden,
+        (b.z_step, 2), (b.pass_on, 2), (b.own_rows, 1), down_in.wait, (exchanged, 0),
         s.first_columns, (s.begin, 0), (s.begin, 1), (s.independent, 0), (s.independent, 1), (b.z_step, 3), b.late,
-        (b.mulz, c, 0), (b.sib_rows, 3), s.z_second, (b.own_rows, 2), s.last_columns, (b.z_step, 4),
-        (b.mulz, c, 1), (b.sib_rows, 2), (s.depend, 0), (s.depend, 1), (s.z_next, 2), (b.sib_z, 2), b.hidden,
+        (b.own_rows, 2), s.z_second, s.last_columns, (b.sib_rows, 4), (b.z_step, 4),
+        (b.mulz, c, 2), (s.depend, 0), (s.depend, 1), (s.z_next, 2), (b.sib_z, 2), b.hidden,
         (exchanged, 1), t.first_columns, (s.second, 2), (t.begin, 0), (s.second, 1, -1, 0), (t.begin, 1),
-        (t.independent, 0), (t.independent, 1), t.last_columns, (s.z_next, 3), t.z_second, s.third, (t.depend, 0), (t.depend, 1),
-        s.z_end, s.fourth, (t.z_next, 2), (t.second, 2), (t.second, 1), (t.z_next, 3), (t.second, -1, 0), t.third, t.z_end,
+        t.last_columns, t.z_second, (s.z_next, 3), s.third, (t.independent, 0), (t.independent, 1), (t.depend, 0), (t.depend, 1),
+        (t.z_next, 2), s.z_end, s.fourth, (t.second, 2), (t.z_next, 3), (t.second, 1, -1, 0), t.third, t.z_end,
         t.fourth, s.finish, t.finish,
     )
     mark("b30_sends")

time: 91 us -> 87.5 us (0.962); the launches traced: 90.8 us -> 86.3 us
  Pallas kernels: 89.3 us -> 84.8 us
    pallas_call x1, Pallas kernels: 89.3 us -> 84.8 us  [local(): pl.pallas_call(kernel, out_shape=jax.ShapeDtypeStruct((64, 448), BF16), i...]
where the time goes in v3:
time: 87.5 us; the launch traced here: 86.3 us
  Pallas kernels  84.8 us (97%)
  local copies, waits for them, and re-layouts  1.47 us (2%)
    pallas_call x1, Pallas kernels, local(): pl.pallas_call(kernel, out_shape=jax.ShapeDtypeStruct((64, 448), BF16), i...  84.8 us

profile of v3, /device:TPU:1, one launch (start us, length us, event | category | flops | bytes accessed | tf_op | source)
XLA Modules:
  0.0 86.3 jit_solution(5103166691916038889)
XLA Ops:
  0.0 84.8 %shard_map.64 = bf16[64,448]{1,0:T(8,128)(2,1)} custom-call(bf16[64,7168]{1,0:T(8,128)(2,1)} %tok.1, f32[8,64]{1,0:T(8,128)} %bitcast.2, s32[8,64]{1,0:T(8,128)} %bitcast.3, bf16[2,7168,128]{2,1,0:T(8,128)(2,1)} %gate_w.1, bf16[2,7168,128]{2,1,0:T(8,128)(2,1)} %up_w.1, bf16[2,128,7168]{2,1,0:T(8,128)(2,1)} %down_w.1), custom_call_target="tpu_custom_call" | custom-call | tf_op jit(solution)/shard_map/pallas_call | solution.py:564
  84.8 1.5 %copy.8 = bf16[64,448]{1,0:T(8,128)(2,1)} copy(bf16[64,448]{1,0:T(8,128)(2,1)} %shard_map.64) | data formatting | bytes 114688
